TPU v7x, 256 devices: a whole 4x4x8 slice. The times are simulated.
256 devices in a mesh: gx: 8 (over y, z_lo), gy: 32 (over z_hi, x, core).
Axes of the slice: x: 4, y: 4, z: 8 (z_hi: 4, z_lo: 2; z = z_hi * 2 + z_lo), core: 2. Of those that a mesh axis runs over, the one named last changes fastest.
Arguments:
- state: float32 [5, 8, 2048, 3072], P(None, None, 'gy', 'gx'), may hold values from -6 to 6
- driving: float32 [5, 8, 2048, 3072], P(None, None, 'gy', 'gx'), may hold values from -6 to 6
- rate: float32 [5, 8], replicated, may hold values from 1 to 6
- sound_square: float32 [8, 2048, 3072], P(None, 'gy', 'gx'), may hold values from 0.3 to 1
Outputs:
- nudged: float32 [5, 8, 2048, 3072], P(None, None, 'gy', 'gx')
All inputs are finite; a program needn't handle non-finite values.
Results may differ from a plain program's by a relative error of at most 0.000064.
Values sent between devices are 32-bit elements; how exact they have to be, the bound alone decides.
A program may use at most 128 MiB of HBM per device.

v0:
```python
import jax
import jax.numpy as jnp
from jax import lax
from jax.sharding import PartitionSpec as P

MODES = 64
SUBSTEPS = 3
GY = "gy"


courant = 0.5


def padded_2(cells, sides, width):
    for axis, dim in sides:
        count = lax.axis_size(axis)
        ends = count - 1
        head = lax.slice_in_dim(cells, 0, width, axis=dim)
        tail = lax.slice_in_dim(cells, cells.shape[dim] - width, cells.shape[dim], axis=dim)
        cells = jnp.concatenate(
            [
                lax.ppermute(tail, axis, [(i, (i + 1) % count) for i in range(ends)]),
                cells,
                lax.ppermute(head, axis, [((i + 1) % count, i) for i in range(ends)]),
            ],
            axis=dim,
        )
    return cells


def tables(count, size, offset, total):
    index = lax.iota(jnp.int32, size) + offset
    order = lax.iota(jnp.int32, count)
    freq = jnp.where(order < count // 2, order, order - count // 2 + 1)
    wrapped = freq[:, None] * (2 * index[None, :] + 1) % (2 * total)
    phase = jnp.pi * wrapped.astype(jnp.float32) / total
    basis = jnp.where(order[:, None] < count // 2, jnp.cos(phase), jnp.sin(phase))
    scaling = jnp.where(order == 0, 1.0 / total, 2.0 / total).astype(jnp.float32)
    return (basis, basis * scaling[:, None])


def vertical(field):
    padded = jnp.pad(field, ((1, 1), (0, 0), (0, 0)))
    return 0.5 * (padded[2:] - padded[:-2])


def inner(field):
    return field[..., 1:-1, 1:-1]


def window_step(fields, sound_square, inside):
    wind_u, wind_v, wind_w, press, theta = fields
    press_x = 0.5 * (press[:, 1:-1, 2:] - press[:, 1:-1, :-2])
    press_y = 0.5 * (press[:, 2:, 1:-1] - press[:, :-2, 1:-1])
    first = inner(inside)
    new_u = (inner(wind_u) - courant * press_x) * first
    new_v = (inner(wind_v) - courant * press_y) * first
    new_w = (inner(wind_w) - courant * vertical(inner(press)) + courant * inner(theta)) * first
    u_x = 0.5 * (new_u[:, 1:-1, 2:] - new_u[:, 1:-1, :-2])
    v_y = 0.5 * (new_v[:, 2:, 1:-1] - new_v[:, :-2, 1:-1])
    diverge = u_x + v_y + vertical(inner(new_w))
    second = inner(first)
    new_p = (inner(inner(press)) - courant * inner(inner(sound_square)) * diverge) * second
    new_t = (inner(inner(theta)) - courant * inner(new_w)) * second
    return (
        (inner(new_u) * second, inner(new_v) * second, inner(new_w) * second, new_p, new_t),
        inner(inner(sound_square)),
        second,
    )


def on_device(state, driving, rate, sound_square):
    high = lax.Precision.HIGHEST
    fields_count, levels, rows, cols = state.shape
    row_start = lax.axis_index(GY) * rows
    col_start = lax.axis_index("gx") * cols
    total_rows = rows * lax.axis_size(GY)
    total_cols = cols * lax.axis_size("gx")
    basis_x, weight_x = tables(MODES, cols, col_start, total_cols)
    basis_y, weight_y = tables(MODES, rows, row_start, total_rows)
    difference = state - driving
    partial_value = jnp.einsum("flyx,kx->flyk", difference, weight_x, precision=high)
    local = jnp.einsum("flyk,jy->fljk", partial_value, weight_y, precision=high)
    modes = lax.psum(local, ("gx", GY))
    scaled = rate[:, :, None, None] * modes
    rows_back = jnp.einsum("fljk,jy->flyk", scaled, basis_y, precision=high)
    tendency = jnp.einsum("flyk,kx->flyx", rows_back, basis_x, precision=high)
    margin = 2 * SUBSTEPS
    packed = jnp.concatenate([state, sound_square[None]], axis=0)
    widened = padded_2(packed, (("gx", 3), (GY, 2)), margin)
    row_ids = lax.iota(jnp.int32, rows + 2 * margin) + row_start - margin
    col_ids = lax.iota(jnp.int32, cols + 2 * margin) + col_start - margin
    row_ok = (row_ids >= 0) & (row_ids < total_rows)
    col_ok = (col_ids >= 0) & (col_ids < total_cols)
    inside = (row_ok[:, None] & col_ok[None, :]).astype(jnp.float32)
    fields = tuple((widened[i] for i in range(fields_count)))
    speeds = widened[fields_count]
    for step in range(SUBSTEPS):
        fields, speeds, inside = window_step(fields, speeds, inside)
    advanced = jnp.stack(fields)
    return advanced - tendency


def solution(mesh):
    return jax.shard_map(
        on_device,
        mesh=mesh,
        in_specs=(P(None, None, GY, "gx"), P(None, None, GY, "gx"), P(), P(None, GY, "gx")),
        out_specs=P(None, None, GY, "gx"),
        check_vma=False,
    )
```

profile of v0, /device:TPU:1, one launch (start us, length us, event | category | flops | bytes accessed | tf_op | source)
XLA Modules:
  0.0 347.5 jit_solution(14394948539552366294)
XLA Ops:
  6.5 0.0 all-reduce.8.cloned.1.call-start
  6.5 2.5 pad_maximum_fusion.2
  9.0 0.5 copy.5
  9.5 4.4 %collective-permute-start = (f32[6,8,64,6]{2,1,3,0:T(8,128)S(1)}, f32[6,8,64,6]{2,1,3,0:T(8,128)S(1)}, u32[]{:S(2)}, u32[]{:S(2)}) collective-permute-start(f32[6,8,64,6]{2,1,3,0:T(8,128)S(1)} %copy.5), channel_id=1, source_target_pairs={{0,32},{32,64},{64,96},{96,128},{128,160},{160,192},{192,224},{1,3... | collective-permute-start | bytes 221192 | tf_op jit(solution)/shard_map/ppermute | solution.py:22
  13.9 0.5 copy.6
  14.5 1.3 collective-permute-start.1
  15.8 0.0 copy-start.6
  15.8 7.6 %fusion = f32[5,8,64,64]{3,2,1,0:T(8,128)S(1)} fusion(f32[5,8,64,384]{3,2,1,0:T(8,128)} %param.4, f32[5,8,64,384]{3,2,1,0:T(8,128)} %param.5, f32[64]{0:T(128)S(1)} %compare_select_fusion, s32[384]{0:T(512)S(1)} %multiply_add_fusion, s32[64]{0:T(128)S(1)} %get-tuple-element.42, pred[64]{0:T(512)(128)(4,1)S(1)} %iota_compare_fusion), kind=kOutput, calls=%fused_computation.1 | convolution fusion | flops 756228096 | bytes 8521792 | tf_op jit(solution)/shard_map/flyx,kx->flyk/dot_general | solution.py:82
  23.4 0.0 copy-done.6
  23.4 2.6 convolution_bitcast_fusion.1
  26.0 0.0 all-reduce.8.cloned.1.call-update
  26.0 0.0 collective-permute-done
  26.0 0.5 copy.7
  26.6 0.0 collective-permute-done.1
  26.6 0.5 copy.8
  27.2 1.9 pad_maximum_fusion.6
  29.0 1.2 copy.9
  30.2 3.9 %collective-permute-start.2 = (f32[6,8,6,396]{3,1,2,0:T(8,128)}, f32[6,8,6,396]{3,1,2,0:T(8,128)}, u32[]{:S(2)}, u32[]{:S(2)}) collective-permute-start(f32[6,8,6,396]{3,1,2,0:T(8,128)} %copy.9), channel_id=1, source_target_pairs={{0,1},{1,2},{2,3},{3,4},{4,5},{5,6},{6,7},{7,8},{8,9},{9,10},{10,1... | collective-permute-start | bytes 1368584 | tf_op jit(solution)/shard_map/ppermute | solution.py:22
  34.2 1.2 copy.10
  35.3 2.3 collective-permute-start.3
  37.6 0.1 and_convert_fusion
  37.7 0.8 slice.380
  38.5 0.1 slice.405
  38.6 0.8 slice.384
  39.4 0.1 slice.434
  39.5 0.8 slice.412
  40.2 0.1 slice.439
  40.3 251.8 %all-reduce.8.cloned.1.call-done = f32[5,8,64,64]{3,2,1,0:T(8,128)} async-done(((f32[5,8,64,64]{3,2,1,0:T(8,128)}), f32[5,8,64,64]{3,2,1,0:T(8,128)}) %all-reduce.8.cloned.1.call-update) | async-done | bytes 655376 | tf_op jit(solution)/shard_map/psum | solution.py:84
  292.1 0.0 copy-done.5
  292.1 2.9 convolution_bitcast_fusion
  295.0 0.0 copy-start.1
  295.0 0.0 collective-permute-done.2
  295.0 1.5 copy.11
  296.5 0.0 collective-permute-done.3
  296.5 1.4 copy.12
  298.0 0.0 copy-done
  298.0 0.0 copy-done.1
  298.0 3.9 %pad_maximum_fusion = f32[6,8,76,396]{3,2,1,0:T(8,128)S(1)} fusion(f32[6,8,6,396]{3,2,1,0:T(8,128)S(1)} %copy.12, f32[6,8,64,6]{3,2,1,0:T(8,128)S(1)} %copy.8, f32[1,8,64,384]{3,2,1,0:T(8,128)S(1)} %bitcast.59, f32[5,8,64,384]{3,2,1,0:T(8,128)S(1)} %copy-done, f32[6,8,64,6]{3,2,1,0:T(8,128)S(1)} %copy.7, f32[6,8,6,396]{3,2,1,0:T(8,128)S(1)} %copy.11), kind=kLoop, calls=%fused_computation | loop fusion | flops 7223040 | bytes 11556864 | tf_op jit(solution)/shard_map/concatenate | solution.py:20
  301.9 0.0 copy-start.2
  301.9 1.5 slice_bitcast_fusion.3
  303.4 0.0 copy-done.2
  303.4 2.3 fusion.7
  305.7 0.3 pad_slice_fusion.1
  306.0 0.5 slice.400
  306.5 0.5 slice.397
  307.0 2.0 fusion.32
  309.0 0.4 slice.424
  309.5 2.4 fusion.113
  311.9 2.1 fusion.39
  313.9 0.3 pad_slice_fusion.7
  314.2 9.2 %slice.428 = f32[8,70,390]{2,1,0:T(8,128)S(1)} slice(f32[8,72,392]{2,1,0:T(8,128)S(1)} %get-tuple-element.9), slice={[0:8], [1:71], [1:391]} | slice | bytes 1747200 | tf_op jit(solution)/shard_map/slice | solution.py:48
  323.4 2.0 fusion.21
  325.4 0.4 slice.446
  325.8 0.0 copy-start.3
  325.8 2.4 fusion.114
  328.2 2.0 fusion.24
  330.3 0.3 pad_slice_fusion.3
  330.6 0.4 slice.450
  331.0 0.3 fusion.63
  331.3 0.3 fusion.61
  331.6 1.1 bitcast_dynamic-update-slice_fusion
  332.7 1.3 fusion.51
  334.0 0.3 fusion.54
  334.3 6.2 %convolution_subtract_fusion = f32[5,8,64,384]{3,2,1,0:T(8,128)} fusion(f32[5,8,64,384]{3,2,1,0:T(8,128)S(1)} %fusion.54, f32[5,8,64,64]{3,2,1,0:T(8,128)S(1)} %convolution_bitcast_fusion, s32[384]{0:T(512)S(1)} %multiply_add_fusion, s32[64]{0:T(128)S(1)} %get-tuple-element.42, pred[64]{0:T(512)(128)(4,1)S(1)} %iota_compare_fusion), kind=kOutput, calls=%fused_computation.3 | convolution fusion | flops 756203520 | bytes 8521536 | tf_op jit(solution)/shard_map/flyk,kx->flyx/dot_general | solution.py:87
  (12 shorter events, 0.1 us)
Async XLA Ops:
  6.5 285.6 %all-reduce.8.cloned.1.call-start = ((), (), s32[]{:S(2)}) async-start(), calls=%async_computation | async-start | bytes 2621440 | tf_op jit(solution)/shard_map/psum | solution.py:84
  9.5 16.5 %collective-permute-start = (f32[6,8,64,6]{2,1,3,0:T(8,128)S(1)}, f32[6,8,64,6]{2,1,3,0:T(8,128)S(1)}, u32[]{:S(2)}, u32[]{:S(2)}) collective-permute-start(f32[6,8,64,6]{2,1,3,0:T(8,128)S(1)} %copy.5), channel_id=1, source_target_pairs={{0,32},{32,64},{64,96},{96,128},{128,160},{160,192},{192,224},{1,3... | collective-permute-start | bytes 221192 | tf_op jit(solution)/shard_map/ppermute | solution.py:22
  14.5 12.2 %collective-permute-start.1 = (f32[6,8,64,6]{2,1,3,0:T(8,128)S(1)}, f32[6,8,64,6]{2,1,3,0:T(8,128)S(1)}, u32[]{:S(2)}, u32[]{:S(2)}) collective-permute-start(f32[6,8,64,6]{2,1,3,0:T(8,128)S(1)} %copy.6), channel_id=1, source_target_pairs={{32,0},{64,32},{96,64},{128,96},{160,128},{192,160},{224,192},{33,... | collective-permute-start | bytes 221192 | tf_op jit(solution)/shard_map/ppermute | solution.py:24
  15.8 7.6 %copy-start.6 = (s32[64]{0:T(128)}, s32[64]{0:T(128)S(1)}, u32[]{:S(2)}) copy-start(s32[64]{0:T(128)S(1)} %get-tuple-element.43) | copy-start | bytes 772
  30.2 264.8 %collective-permute-start.2 = (f32[6,8,6,396]{3,1,2,0:T(8,128)}, f32[6,8,6,396]{3,1,2,0:T(8,128)}, u32[]{:S(2)}, u32[]{:S(2)}) collective-permute-start(f32[6,8,6,396]{3,1,2,0:T(8,128)} %copy.9), channel_id=1, source_target_pairs={{0,1},{1,2},{2,3},{3,4},{4,5},{5,6},{6,7},{7,8},{8,9},{9,10},{10,1... | collective-permute-start | bytes 1368584 | tf_op jit(solution)/shard_map/ppermute | solution.py:22
  35.3 256.8 %copy-start.5 = (f32[5,8]{1,0:T(8,128)S(1)}, f32[5,8]{1,0:T(8,128)}, u32[]{:S(2)}) copy-start(f32[5,8]{1,0:T(8,128)} %param.6) | copy-start | bytes 484
  35.3 261.2 %collective-permute-start.3 = (f32[6,8,6,396]{3,1,2,0:T(8,128)}, f32[6,8,6,396]{3,1,2,0:T(8,128)}, u32[]{:S(2)}, u32[]{:S(2)}) collective-permute-start(f32[6,8,6,396]{3,1,2,0:T(8,128)} %copy.10), channel_id=1, source_target_pairs={{1,0},{2,1},{3,2},{4,3},{5,4},{6,5},{7,6},{8,7},{9,8},{10,9},{11,1... | collective-permute-start | bytes 1368584 | tf_op jit(solution)/shard_map/ppermute | solution.py:24
  292.1 5.9 %copy-start = (f32[5,8,64,384]{3,2,1,0:T(8,128)S(1)}, f32[5,8,64,384]{3,2,1,0:T(8,128)}, u32[]{:S(2)}) copy-start(f32[5,8,64,384]{3,2,1,0:T(8,128)} %param.4) | copy-start | bytes 11796484
  295.0 3.0 copy-start.1
  301.9 1.5 copy-start.2
  309.4 2.4 copy-start.4
  325.8 2.4 copy-start.3
Sparse Core Ops, SparseCore 0:
  26.1 265.9 all-reduce.7
where the time goes:
time: 350 us; the launch traced here: 348 us
  waiting for transfers between devices  252 us (72%)
  other arithmetic  26.8 us (8%)
  local copies, waits for them, and re-layouts  23.8 us (7%)
  matrix products  19.2 us (5%)
  between operations  14 us (4%)
  starting transfers between devices  11.9 us (3%)
    psum x1, waiting for transfers between devices, on_device(): modes = lax.psum(local, ('gx', GY))  252 us
    slice x12, local copies, waits for them, and re-layouts, inner(): return field[..., 1:-1, 1:-1]  14 us
    ppermute x2, starting transfers between devices, padded_2(): lax.ppermute(tail, axis, [(i, (i + 1) % count) for i in range(ends)])  8.31 us
    dot_general x1, matrix products, on_device(): jnp.einsum('flyx,kx->flyk', difference, weight_x, precision=high)  7.58 us
  transfers between devices with their start and end apart: 5, of which 1 were waited for; matrix products, arithmetic and copies ran while one was open for 7% of the time, Pallas kernels for 0%

commit v1 on v0

v1 whole, which is shorter than its diff:
```python
import jax
import jax.numpy as jnp
import numpy as np
from jax import lax
from jax.experimental import pallas as pl
from jax.experimental.pallas import tpu as pltpu
from jax.sharding import PartitionSpec as P

MODES = 64
SUBSTEPS = 3
NX = 3072
NY = 2048
NF, NL, ROWS, COLS = 5, 8, 64, 384
GX, GY = 8, 32
F32, BF16 = jnp.float32, jnp.bfloat16
MESH = pl.DeviceIdType.MESH
TOP, BOT = 16, 80
HALF, CHUNK = 640, 40
U, V, W, PR, TH, SS = range(6)


def basis(size):
    index = np.arange(size, dtype=np.int64)
    order = np.arange(MODES, dtype=np.int64)
    freq = np.where(order < MODES // 2, order, order - MODES // 2 + 1)
    wrapped = (freq[:, None] * (2 * index[None, :] + 1)) % (2 * size)
    phase = np.float32(np.pi) * wrapped.astype(np.float32) / np.float32(size)
    phase = phase.astype(np.float64)
    table = np.where(order[:, None] < MODES // 2, np.cos(phase), np.sin(phase))
    scaling = np.where(order == 0, 1.0 / size, 2.0 / size).astype(np.float32)
    table = table.astype(np.float32)
    return table, table * scaling[:, None]


def tables():
    basis_x, _ = basis(NX)
    basis_y, weight_y = basis(NY)
    tab_x = basis_x.reshape(MODES, GX, COLS).transpose(1, 0, 2)
    by_tile = basis_y.reshape(MODES, GY, ROWS).transpose(1, 2, 0)
    wy_tile = weight_y.reshape(MODES, GY, ROWS).transpose(1, 0, 2)
    return np.ascontiguousarray(tab_x), np.concatenate([wy_tile, by_tile], axis=2)


def lanes(shape):
    return lax.broadcasted_iota(jnp.int32, shape, len(shape) - 1)


def split(x):
    high = x.astype(BF16)
    return high, (x - high.astype(F32)).astype(BF16)


def y_table(pair):
    lane = lanes(pair.shape)
    high = pair.astype(BF16).astype(F32)
    first = jnp.where(lane < 64, high, pair - high)
    second = jnp.where(lane < 64, high, 0.0)
    return jnp.concatenate([first, second], axis=1).astype(BF16)


def dot(a, b):
    return jnp.dot(a, b, preferred_element_type=F32)


def mode_kernel(
    state, driving, sound, tab_x, tab_y,
    modes, adv, xt3, yt3,
    big, drv, tx, ty, wx, wy, mask, local, half, core_recv, xy_recv, red, z_recv,
    xs, xr, ys, yr, cs, cr,
    ld_sem, drv_sem, snd_sem, tab_sem, core_sem, xy_send, xy_got, z_send, z_got,
    ag_send, ag_got, fw_send, fw_got, xh_send, xh_got, yh_send, yh_got, ch_send, ch_got, out_sem,
):
    gx, gy = lax.axis_index("gx"), lax.axis_index("gy")
    py, zlo = gx // 2, gx % 2
    core, px, zhi = gy % 2, (gy // 2) % 4, gy // 8
    pz = zhi * 2 + zlo
    me = py * 4 + px

    def at(x, y, z, c):
        return {"gx": y * 2 + z % 2, "gy": ((z // 2) * 4 + x) * 2 + c}

    partner = at(px, py, pz, 1 - core)

    def plane(d):
        return (px + d % 4) % 4, (py + d // 4) % 4

    def plane_dev(d):
        x, y = plane(d)
        return at(x, y, pz, core)

    def column_dev(d):
        return at(px, py, (pz + d) % 8, core)

    left, right = {"gx": (gx + GX - 1) % GX, "gy": gy}, {"gx": (gx + 1) % GX, "gy": gy}
    above, below = {"gx": gx, "gy": (gy + GY - 1) % GY}, {"gx": gx, "gy": (gy + 1) % GY}
    sides = (left, right)
    rows_to = (above, below)

    far = sorted(range(1, 16), key=lambda d: -(min(d % 4, 4 - d % 4) + min(d // 4, 4 - d // 4)))
    deep = sorted(range(1, 8), key=lambda d: -min(d, 8 - d))

    barrier = pltpu.get_barrier_semaphore()
    peers = [partner] + [plane_dev(d) for d in far] + [column_dev(d) for d in deep]
    peers += [left, right, above, below]
    for peer in peers:
        pl.semaphore_signal(barrier, inc=1, device_id=peer, device_id_type=MESH)

    def remote(src, dst, send, recv, dev):
        return pltpu.make_async_remote_copy(
            src_ref=src, dst_ref=dst, send_sem=send, recv_sem=recv, device_id=dev, device_id_type=MESH
        )

    def load(f, t):
        return pltpu.make_async_copy(
            state.at[f, :, :, pl.ds(t * 128, 128)], big.at[f, :, t, pl.ds(TOP, ROWS), :], ld_sem.at[f, t]
        )

    def load_drv(f):
        return pltpu.make_async_copy(driving.at[f], drv.at[f], drv_sem.at[f])

    def load_sound(t):
        return pltpu.make_async_copy(
            sound.at[:, :, pl.ds(t * 128, 128)], big.at[SS, :, t, pl.ds(TOP, ROWS), :], snd_sem.at[t]
        )

    get_tx = pltpu.make_async_copy(tab_x.at[gx], tx, tab_sem.at[0])
    get_ty = pltpu.make_async_copy(tab_y.at[gy], ty, tab_sem.at[1])
    get_tx.start()
    get_ty.start()
    for f in range(NF):
        for t in range(3):
            load(f, t).start()
        load_drv(f).start()
    for t in range(3):
        load_sound(t).start()

    get_tx.wait()
    get_ty.wait()
    b_x = tx[...]
    k_row = lax.broadcasted_iota(jnp.int32, b_x.shape, 0)
    w_x = b_x * jnp.where(k_row == 0, np.float32(1.0 / NX), np.float32(2.0 / NX))
    w_hi, w_lo = split(w_x)
    wx[...] = jnp.concatenate([w_hi, w_hi, w_lo, w_lo], axis=0)
    b_hi, b_lo = split(b_x)
    xt3[...] = jnp.concatenate([b_hi, b_hi, b_hi, b_hi, b_lo, b_lo], axis=0)
    pair = ty[...]
    lane2 = lanes(pair.shape)
    turned = pltpu.roll(pair, 64, 1)
    wy[...] = y_table(jnp.where(lane2 < 64, pair, turned))
    yt3[...] = y_table(jnp.where(lane2 < 64, turned, pair))

    row = lax.broadcasted_iota(jnp.int32, (96, 128), 0)
    lane = lanes((96, 128))
    row_ok = ((row >= TOP) | (gy > 0)) & ((row < BOT) | (gy < GY - 1))
    col_ok = jnp.where(lane < 64, jnp.where(gx < GX - 1, 1.0, 0.0), jnp.where(gx > 0, 1.0, 0.0))
    row_ok = jnp.where(row_ok, 1.0, 0.0)
    for t in range(3):
        mask[t] = row_ok
    mask[3] = row_ok * col_ok

    def project(f, _):
        for t in range(3):
            load(f, t).wait()
        load_drv(f).wait()
        diff = jnp.concatenate(
            [
                big[f, :, t, TOP:BOT, :].reshape(512, 128)
                - drv[f, :, :, t * 128 : (t + 1) * 128].reshape(512, 128)
                for t in range(3)
            ],
            axis=1,
        )
        high, low = split(diff)
        nt = (((1,), (1,)), ((), ()))
        a = lax.dot_general(high, wx[...], nt, preferred_element_type=F32)
        b = lax.dot_general(low, wx[0:128], nt, preferred_element_type=F32)
        part = a[:, :128] + (a[:, 128:] + b)
        side = lanes((64, 128))
        pairs = [
            jnp.where(side < 64, part[128 * q : 128 * q + 64], part[128 * q + 64 : 128 * q + 128])
            for q in range(4)
        ]
        high, low = split(jnp.concatenate(pairs, axis=1))
        rhs = jnp.concatenate([high, high, low, low], axis=0)
        out = dot(wy[...], rhs)
        for q in range(4):
            local[pl.ds(pl.multiple_of((f * 4 + q) * 64, 64), 64), :] = out[:, 128 * q : 128 * q + 128]
        return 0

    lax.fori_loop(0, NF, project, 0)
    pl.semaphore_wait(barrier, len(peers))

    give = remote(
        local.at[pl.ds(pl.multiple_of((1 - core) * HALF, 8), HALF), :], core_recv, core_sem.at[0], core_sem.at[1], partner
    )
    give.start()

    for t in range(3):
        load_sound(t).wait()
    slot = lanes((32, 128)) // 8

    def pack_x(f, _):
        for side, tile in ((0, 0), (1, 2)):
            acc = None
            for i in range(16):
                cells = big[f, i // 2, tile, TOP + 32 * (i % 2) : TOP + 32 * (i % 2) + 32, :]
                shift = (8 * (i + side)) % 128
                cells = pltpu.roll(cells, shift, 1) if shift else cells
                acc = cells if acc is None else jnp.where(slot == i, cells, acc)
            xs[side, f] = acc
        return 0

    lax.fori_loop(0, 6, pack_x, 0)
    x_copies = [remote(xs.at[s], xr.at[s], xh_send.at[s], xh_got.at[s], sides[s]) for s in range(2)]
    for copy in x_copies:
        copy.start()

    give.wait()
    half[...] = local[pl.ds(pl.multiple_of(core * HALF, 8), HALF), :] + core_recv[...]

    def scatter(d):
        x, y = plane(d)
        return remote(
            half.at[pl.ds(pl.multiple_of((y * 4 + x) * CHUNK, 8), CHUNK), :],
            xy_recv.at[d], xy_send.at[d], xy_got.at[d], plane_dev(d),
        )

    for d in far:
        scatter(d).start()

    low_rows = lax.broadcasted_iota(jnp.int32, (3, 8, 128), 1) < 4

    def pack_y(l, _):
        for s, r in ((0, TOP), (1, BOT - 8)):
            def strip(f):
                return big[f, l, 0:3, r : r + 8, :]

            def joined(a, b):
                if s == 0:
                    return jnp.where(low_rows, strip(a), pltpu.roll(strip(b), 4, 1))
                return jnp.where(low_rows, pltpu.roll(strip(a), 4, 1), strip(b))

            ys[s, l, 0] = strip(PR)
            ys[s, l, 1] = strip(V)
            ys[s, l, 2] = joined(U, W)
            ys[s, l, 3] = joined(TH, SS)
        return 0

    lax.fori_loop(0, NL, pack_y, 0)
    y_copies = [remote(ys.at[s], yr.at[s], yh_send.at[s], yh_got.at[s], rows_to[s]) for s in range(2)]
    for copy in y_copies:
        copy.start()

    for copy in x_copies:
        copy.wait()
    near = lanes((32, 128)) < 64

    def unpack_x(f, _):
        for i in range(16):
            shift_a, shift_b = (128 - 8 * i) % 128, (128 - 8 * (i + 1)) % 128
            a, b = xr[0, f], xr[1, f]
            a = pltpu.roll(a, shift_a, 1) if shift_a else a
            b = pltpu.roll(b, shift_b, 1) if shift_b else b
            r = TOP + 32 * (i % 2)
            big[f, i // 2, 3, r : r + 32, :] = jnp.where(near, a, b)
        return 0

    lax.fori_loop(0, 6, unpack_x, 0)

    slot8 = lanes((8, 128)) // 16

    def pack_c(f, _):
        for s, r in ((0, TOP), (1, BOT - 8)):
            acc = None
            for l in range(NL):
                shift = (8 + 16 * l) % 128
                cells = pltpu.roll(big[f, l, 3, r : r + 8, :], shift, 1)
                acc = cells if acc is None else jnp.where(slot8 == l, cells, acc)
            cs[s, f] = acc
        return 0

    lax.fori_loop(0, 6, pack_c, 0)
    c_copies = [remote(cs.at[s], cr.at[s], ch_send.at[s], ch_got.at[s], rows_to[s]) for s in range(2)]
    for copy in c_copies:
        copy.start()

    for d in far:
        scatter(d).wait_recv()
    total = half[pl.ds(pl.multiple_of(me * CHUNK, 8), CHUNK), :]
    for d in range(1, 16):
        total = total + xy_recv[d]
    red[...] = total

    def across(d):
        return remote(red, z_recv.at[d], z_send.at[d], z_got.at[d], column_dev(d))

    for d in deep:
        across(d).start()
    for d in deep:
        across(d).wait_recv()
    total = red[...]
    for d in range(1, 8):
        total = total + z_recv[d]

    def chunk_of(q):
        return modes.at[pl.ds(pl.multiple_of(core * HALF + q * CHUNK, 8), CHUNK), :]

    modes[pl.ds(pl.multiple_of(core * HALF + me * CHUNK, 8), CHUNK), :] = total

    def gather(d):
        return remote(chunk_of(me), chunk_of(me), ag_send.at[d], ag_got.at[d], plane_dev(d))

    def forward(d):
        x, y = (px + 4 - d % 4) % 4, (py + 4 - d // 4) % 4
        ref = chunk_of(y * 4 + x)
        return remote(ref, ref, fw_send.at[d], fw_got.at[d], partner)

    for d in far:
        gather(d).start()
    forward(0).start()

    for copy in y_copies:
        copy.wait()
    for copy in c_copies:
        copy.wait()

    def unpack_y(l, _):
        for s, r in ((0, BOT), (1, TOP - 8)):
            def put(f, cells):
                big[f, l, 0:3, r : r + 8, :] = cells

            def other(cells):
                return pltpu.roll(cells, 4, 1)

            put(PR, yr[s, l, 0] * mask[0:3, r : r + 8, :])
            put(V, yr[s, l, 1])
            one, two = yr[s, l, 2], yr[s, l, 3]
            if s == 0:
                put(U, one)
                put(W, other(one))
                put(TH, two)
                put(SS, other(two))
            else:
                put(U, other(one))
                put(W, one)
                put(TH, other(two))
                put(SS, two)
        return 0

    lax.fori_loop(0, NL, unpack_y, 0)

    def unpack_c(f, _):
        for s, r in ((0, BOT), (1, TOP - 8)):
            for l in range(NL):
                big[f, l, 3, r : r + 8, :] = pltpu.roll(cr[s, f], (128 - 8 - 16 * l) % 128, 1)
        return 0

    lax.fori_loop(0, 6, unpack_c, 0)

    def mask_p(l, _):
        big[PR, l, 3, 8:88, :] = big[PR, l, 3, 8:88, :] * mask[3, 8:88, :]
        return 0

    lax.fori_loop(0, NL, mask_p, 0)

    lane4 = lanes((4, 16, 128))
    at_end, at_start = lane4 == 127, lane4 == 0

    def across_x(c):
        fwd, back = pltpu.roll(c, 127, 2), pltpu.roll(c, 1, 2)
        fwd = jnp.where(at_end, jnp.concatenate([fwd[1:], fwd[:1]], axis=0), fwd)
        back = jnp.where(at_start, jnp.concatenate([back[3:], back[:3]], axis=0), back)
        return fwd - back

    def get(f, l, r):
        return big[f, l, :, r : r + 16, :]

    def vertical(f, l, r):
        up = get(f, jnp.minimum(l + 1, NL - 1), r) * jnp.where(l < NL - 1, 1.0, 0.0)
        down = get(f, jnp.maximum(l - 1, 0), r) * jnp.where(l > 0, 1.0, 0.0)
        return up - down

    def winds(l, _):
        for r in range(8, 88, 16):
            ok = mask[:, r : r + 16, :]
            big[U, l, :, r : r + 16, :] = (get(U, l, r) - 0.25 * across_x(get(PR, l, r))) * ok
            along = get(PR, l, r + 1) - get(PR, l, r - 1)
            big[V, l, :, r : r + 16, :] = (get(V, l, r) - 0.25 * along) * ok
            big[W, l, :, r : r + 16, :] = get(W, l, r) - 0.25 * vertical(PR, l, r) + 0.5 * get(TH, l, r)
        return 0

    def pressure(rows):
        def body(l, _):
            for r in rows:
                along = get(V, l, r + 1) - get(V, l, r - 1)
                diverge = across_x(get(U, l, r)) + along + vertical(W, l, r)
                new_p = (get(PR, l, r) - 0.25 * get(SS, l, r) * diverge) * mask[:, r : r + 16, :]
                big[PR, l, :, r : r + 16, :] = new_p
                big[TH, l, :, r : r + 16, :] = get(TH, l, r) - 0.5 * get(W, l, r)
            return 0

        return body

    def put_out(first, count, t, k):
        return pltpu.make_async_copy(
            big.at[pl.ds(first, count), :, t, pl.ds(TOP, ROWS), :],
            adv.at[pl.ds(first, count), :, :, pl.ds(t * 128, 128)],
            out_sem.at[k, t],
        )

    for step in range(SUBSTEPS):
        last = step == SUBSTEPS - 1
        lax.fori_loop(0, NL, winds, 0)
        if last:
            for t in range(3):
                put_out(0, 3, t, 0).start()
            for d in far:
                gather(d).wait_recv()
                forward(d).start()
        lax.fori_loop(0, NL, pressure(range(TOP, BOT, 16) if last else range(8, 88, 16)), 0)
    for t in range(3):
        put_out(3, 2, t, 1).start()

    for d in range(16):
        forward(d).wait()
    for d in far:
        scatter(d).wait_send()
        gather(d).wait_send()
    for d in deep:
        across(d).wait_send()
    for t in range(3):
        put_out(0, 3, t, 0).wait()
        put_out(3, 2, t, 1).wait()


def sum_modes(state, driving, sound, tab_x, tab_y):
    vmem = pl.BlockSpec(memory_space=pltpu.VMEM)
    hbm = pl.BlockSpec(memory_space=pl.ANY)
    dma = pltpu.SemaphoreType.DMA
    return pl.pallas_call(
        mode_kernel,
        out_shape=(
            jax.ShapeDtypeStruct((2 * HALF, 128), F32),
            jax.ShapeDtypeStruct((NF, NL, ROWS, COLS), F32),
            jax.ShapeDtypeStruct((384, COLS), BF16),
            jax.ShapeDtypeStruct((64, 256), BF16),
        ),
        in_specs=[hbm] * 5,
        out_specs=(vmem, hbm, vmem, vmem),
        scratch_shapes=[
            pltpu.VMEM((6, NL, 4, 96, 128), F32),
            pltpu.VMEM((NF, NL, ROWS, COLS), F32),
            pltpu.VMEM((MODES, COLS), F32),
            pltpu.VMEM((64, 128), F32),
            pltpu.VMEM((256, COLS), BF16),
            pltpu.VMEM((64, 256), BF16),
            pltpu.VMEM((4, 96, 128), F32),
            pltpu.VMEM((2 * HALF, 128), F32),
            pltpu.VMEM((HALF, 128), F32),
            pltpu.VMEM((HALF, 128), F32),
            pltpu.VMEM((16, CHUNK, 128), F32),
            pltpu.VMEM((CHUNK, 128), F32),
            pltpu.VMEM((8, CHUNK, 128), F32),
            pltpu.VMEM((2, 6, 32, 128), F32),
            pltpu.VMEM((2, 6, 32, 128), F32),
            pltpu.VMEM((2, NL, 4, 3, 8, 128), F32),
            pltpu.VMEM((2, NL, 4, 3, 8, 128), F32),
            pltpu.VMEM((2, 6, 8, 128), F32),
            pltpu.VMEM((2, 6, 8, 128), F32),
            dma((NF, 3)), dma((NF,)), dma((3,)), dma((2,)), dma((2,)),
            dma((16,)), dma((16,)), dma((8,)), dma((8,)),
            dma((16,)), dma((16,)), dma((16,)), dma((16,)),
            dma((2,)), dma((2,)), dma((2,)), dma((2,)), dma((2,)), dma((2,)), dma((2, 3)),
        ],
        compiler_params=pltpu.CompilerParams(
            collective_id=0, has_side_effects=True, vmem_limit_bytes=48 * 1024 * 1024
        ),
        name="sum_modes",
    )(state, driving, sound, tab_x, tab_y)


def back_kernel(rate, modes, xt3, yt3, adv, out):
    f = pl.program_id(0)
    side = lanes((64, 128)) < 64
    scaled = [modes[q] * jnp.where(side, rate[f, 2 * q], rate[f, 2 * q + 1]) for q in range(4)]
    high, low = split(jnp.concatenate(scaled, axis=1))
    back = dot(yt3[...], jnp.concatenate([high, high, low, low], axis=0))
    rows = []
    for q in range(4):
        both = back[:, 128 * q : 128 * q + 128]
        rows += [jnp.where(side, both, 0.0), jnp.where(side, 0.0, both)]
    high, low = split(jnp.concatenate(rows, axis=0))
    tendency = dot(jnp.concatenate([high, low, high], axis=1), xt3[...])
    out[0] = adv[0] - tendency.reshape(NL, ROWS, COLS)


def nudge(rate, modes, xt3, yt3, adv):
    block = pl.BlockSpec((1, NL, ROWS, COLS), lambda f: (f, 0, 0, 0))
    vmem = pl.BlockSpec(memory_space=pltpu.VMEM)
    return pl.pallas_call(
        back_kernel,
        grid=(NF,),
        out_shape=jax.ShapeDtypeStruct((NF, NL, ROWS, COLS), F32),
        in_specs=[
            pl.BlockSpec(memory_space=pltpu.SMEM),
            pl.BlockSpec((4, 64, 128), lambda f: (f, 0, 0)),
            vmem,
            vmem,
            block,
        ],
        out_specs=block,
        compiler_params=pltpu.CompilerParams(
            dimension_semantics=("arbitrary",), vmem_limit_bytes=24 * 1024 * 1024
        ),
        name="nudge",
    )(rate, modes, xt3, yt3, adv)


def solution(mesh):
    tab_x, tab_y = tables()

    def on_device(state, driving, rate, sound_square):
        modes, adv, xt3, yt3 = sum_modes(state, driving, sound_square, jnp.asarray(tab_x), jnp.asarray(tab_y))
        return nudge(rate, modes.reshape(20, 64, 128), xt3, yt3, adv)

    return jax.shard_map(
        on_device,
        mesh=mesh,
        in_specs=(P(None, None, "gy", "gx"), P(None, None, "gy", "gx"), P(), P(None, "gy", "gx")),
        out_specs=P(None, None, "gy", "gx"),
        check_vma=False,
    )
```

time: 350 us -> 53.5 us (0.15)
  waiting for transfers between devices: 252 us -> 0 us
  Pallas kernels: 0 us -> 47.6 us
  other arithmetic: 26.8 us -> 0 us
  matrix products: 19.2 us -> 0 us
  local copies, waits for them, and re-layouts: 23.8 us -> 5.6 us
  between operations: 14 us -> 0.03 us
  starting transfers between devices: 11.9 us -> 0 us
    psum x1 -> x0, waiting for transfers between devices: 252 us -> none  [on_device(): modes = lax.psum(local, ('gx', GY))]
    pallas_call x0 -> x2, Pallas kernels: none -> 47.6 us  [the longest x1 42.7 us: sum_modes(): pl.pallas_call(mode_kernel, out_shape=(jax.ShapeDtypeStruct((2 * HALF, 12...]
    dot_general x4 -> x0, matrix products: 19.2 us -> none  [the longest x1 7.58 us: on_device(): jnp.einsum('flyx,kx->flyk', difference, weight_x, precision=high)]
    slice x19 -> x0, local copies, waits for them, and re-layouts: 18.3 us -> none  [the longest x12 14 us: inner(): return field[..., 1:-1, 1:-1]]
    ppermute x4 -> x0, starting transfers between devices: 11.9 us -> none  [the longest x2 8.31 us: padded_2(): lax.ppermute(tail, axis, [(i, (i + 1) % count) for i in range(ends)])]
    mul x5 -> x0, other arithmetic: 10.4 us -> none  [the longest x2 4.34 us: window_step(): new_u = (inner(wind_u) - courant * press_x) * first]
    slice x4 -> x0, other arithmetic: 9.08 us -> none  [the longest x2 4.75 us: inner(): return field[..., 1:-1, 1:-1]]
    unnamed x14 -> x10, local copies, waits for them, and re-layouts: 0.03 us -> 5.6 us
  transfers between devices with their start and end apart: 5 -> 0, of which waited for: 1 -> 0; matrix products, arithmetic and copies ran while one was open for 7% -> 0% of each run, Pallas kernels for 0% -> 0%
where the time goes in v1:
time: 53.5 us; the launch traced here: 53.3 us
  Pallas kernels  47.6 us (89%)
  local copies, waits for them, and re-layouts  5.6 us (10%)
    pallas_call x1, Pallas kernels, sum_modes(): pl.pallas_call(mode_kernel, out_shape=(jax.ShapeDtypeStruct((2 * HALF, 12...  42.7 us
    unnamed x10, local copies, waits for them, and re-layouts  5.6 us
    pallas_call x1, Pallas kernels, nudge(): pl.pallas_call(back_kernel, grid=(NF,), out_shape=jax.ShapeDtypeStruct((N...  4.94 us

profile of v1, /device:TPU:1, one launch (start us, length us, event | category | flops | bytes accessed | tf_op | source)
XLA Modules:
  0.0 53.3 jit_solution(15233435976262042274)
XLA Ops:
  0.0 0.0 copy-start.1
  0.0 1.2 %copy-done.1 = f32[32,64,128]{2,1,0:T(8,128)S(1)} copy-done((f32[32,64,128]{2,1,0:T(8,128)S(1)}, f32[32,64,128]{2,1,0:T(8,128)}, u32[]{:S(2)}) %copy-start.1) | copy-done | bytes 1048600
  1.2 0.0 copy-start.2
  1.2 1.1 %copy-done.2 = f32[8,64,384]{2,1,0:T(8,128)S(1)} copy-done((f32[8,64,384]{2,1,0:T(8,128)S(1)}, f32[8,64,384]{2,1,0:T(8,128)}, u32[]{:S(2)}) %copy-start.2) | copy-done | bytes 786456
  2.4 0.0 copy-start.3
  2.4 1.1 %copy-done.3 = f32[8,64,384]{2,1,0:T(8,128)S(1)} copy-done((f32[8,64,384]{2,1,0:T(8,128)S(1)}, f32[8,64,384]{2,1,0:T(8,128)}, u32[]{:S(2)}) %copy-start.3) | copy-done | bytes 786456
  3.5 0.0 copy-start.4
  3.5 42.7 %sum_modes.1 = (f32[1280,128]{1,0:T(8,128)S(1)}, f32[5,8,64,384]{3,2,1,0:T(8,128)}, bf16[384,384]{1,0:T(8,128)(2,1)S(1)}, bf16[64,256]{1,0:T(8,128)(2,1)S(1)}) custom-call(f32[5,8,64,384]{3,2,1,0:T(8,128)} %state.1, f32[5,8,64,384]{3,2,1,0:T(8,128)} %driving.1, f32[8,64,384]{2,1,0:T(8,128)S(1)} %copy-done.2, f32[8,64,384]{2,1,0:T(8,128)S(1)} %copy-done.3, ...), custom_call_target="tpu_custom_call" | custom-call | tf_op jit(solution)/shard_map/sum_modes/pallas_call | solution.py:440
  46.2 0.0 copy-done.4
  46.2 0.0 copy-start
  46.2 2.1 %copy-done = f32[5,8,64,384]{3,2,1,0:T(8,128)S(1)} copy-done((f32[5,8,64,384]{3,2,1,0:T(8,128)S(1)}, f32[5,8,64,384]{3,2,1,0:T(8,128)}, u32[]{:S(2)}) %copy-start) | copy-done | bytes 3932184
  48.3 4.9 %nudge.1 = f32[5,8,64,384]{3,2,1,0:T(8,128)} custom-call(f32[5,8]{1,0:T(8,128)S(1)} %copy-done.4, f32[20,64,128]{2,1,0:T(8,128)S(1)} %bitcast.1, bf16[384,384]{1,0:T(8,128)(2,1)S(1)} %get-tuple-element.10.xt3, bf16[64,256]{1,0:T(8,128)(2,1)S(1)} %get-tuple-element.11.yt3, f32[5,8,64,384]{3,2,1,0:T(8,128)S(1)} %copy-done), custom_call_target="tpu_custom_call" | custom-call | tf_op jit(solution)/shard_map/nudge/pallas_call | solution.py:500
Async XLA Ops:
  0.0 1.2 %copy-start.1 = (f32[32,64,128]{2,1,0:T(8,128)S(1)}, f32[32,64,128]{2,1,0:T(8,128)}, u32[]{:S(2)}) copy-start(f32[32,64,128]{2,1,0:T(8,128)} %constant.5.clone.tab_y) | copy-start | bytes 3145732
  1.2 1.1 %copy-start.2 = (f32[8,64,384]{2,1,0:T(8,128)S(1)}, f32[8,64,384]{2,1,0:T(8,128)}, u32[]{:S(2)}) copy-start(f32[8,64,384]{2,1,0:T(8,128)} %sound.1) | copy-start | bytes 2359300
  2.4 1.1 %copy-start.3 = (f32[8,64,384]{2,1,0:T(8,128)S(1)}, f32[8,64,384]{2,1,0:T(8,128)}, u32[]{:S(2)}) copy-start(f32[8,64,384]{2,1,0:T(8,128)} %constant.4.clone.tab_x) | copy-start | bytes 2359300
  3.5 42.7 %copy-start.4 = (f32[5,8]{1,0:T(8,128)S(1)}, f32[5,8]{1,0:T(8,128)}, u32[]{:S(2)}) copy-start(f32[5,8]{1,0:T(8,128)} %rate.1) | copy-start | bytes 484
  46.2 2.1 %copy-start = (f32[5,8,64,384]{3,2,1,0:T(8,128)S(1)}, f32[5,8,64,384]{3,2,1,0:T(8,128)}, u32[]{:S(2)}) copy-start(f32[5,8,64,384]{3,2,1,0:T(8,128)} %get-tuple-element.12.adv) | copy-start | bytes 11796484

commit v2 on v1

--- a/solution.py
+++ b/solution.py
@@ -68,7 +68,7 @@
     big, drv, tx, ty, wx, wy, mask, local, half, core_recv, xy_recv, red, z_recv,
     xs, xr, ys, yr, cs, cr,
     ld_sem, drv_sem, snd_sem, tab_sem, core_sem, xy_send, xy_got, z_send, z_got,
-    ag_send, ag_got, fw_send, fw_got, xh_send, xh_got, yh_send, yh_got, ch_send, ch_got, out_sem,
+    ag_send, ag_got, fw_send, fw_got, xh_send, xh_got, yh_send, yh_got, ch_send, ch_got,
 ):
     gx, gy = lax.axis_index("gx"), lax.axis_index("gy")
     py, zlo = gx // 2, gx % 2
@@ -127,10 +127,13 @@
     get_ty = pltpu.make_async_copy(tab_y.at[gy], ty, tab_sem.at[1])
     get_tx.start()
     get_ty.start()
-    for f in range(NF):
+    def nth(i):
+        return jnp.where(core == 0, NF - 1 - i, i)
+
+    for i in range(NF):
         for t in range(3):
-            load(f, t).start()
-        load_drv(f).start()
+            load(nth(i), t).start()
+        load_drv(nth(i)).start()
     for t in range(3):
         load_sound(t).start()
 
@@ -158,7 +161,8 @@
         mask[t] = row_ok
     mask[3] = row_ok * col_ok
 
-    def project(f, _):
+    def project(i, _):
+        f = nth(i)
         for t in range(3):
             load(f, t).wait()
         load_drv(f).wait()
@@ -187,13 +191,14 @@
             local[pl.ds(pl.multiple_of((f * 4 + q) * 64, 64), 64), :] = out[:, 128 * q : 128 * q + 128]
         return 0
 
-    lax.fori_loop(0, NF, project, 0)
+    lax.fori_loop(0, 3, project, 0)
     pl.semaphore_wait(barrier, len(peers))
 
     give = remote(
         local.at[pl.ds(pl.multiple_of((1 - core) * HALF, 8), HALF), :], core_recv, core_sem.at[0], core_sem.at[1], partner
     )
     give.start()
+    lax.fori_loop(3, NF, project, 0)
 
     for t in range(3):
         load_sound(t).wait()
@@ -211,10 +216,6 @@
         return 0
 
     lax.fori_loop(0, 6, pack_x, 0)
-    x_copies = [remote(xs.at[s], xr.at[s], xh_send.at[s], xh_got.at[s], sides[s]) for s in range(2)]
-    for copy in x_copies:
-        copy.start()
-
     give.wait()
     half[...] = local[pl.ds(pl.multiple_of(core * HALF, 8), HALF), :] + core_recv[...]
 
@@ -228,6 +229,10 @@
     for d in far:
         scatter(d).start()
 
+    x_copies = [remote(xs.at[s], xr.at[s], xh_send.at[s], xh_got.at[s], sides[s]) for s in range(2)]
+    for copy in x_copies:
+        copy.start()
+
     low_rows = lax.broadcasted_iota(jnp.int32, (3, 8, 128), 1) < 4
 
     def pack_y(l, _):
@@ -250,6 +255,67 @@
     y_copies = [remote(ys.at[s], yr.at[s], yh_send.at[s], yh_got.at[s], rows_to[s]) for s in range(2)]
     for copy in y_copies:
         copy.start()
+
+    lane4 = lanes((4, 16, 128))
+    at_end, at_start = lane4 == 127, lane4 == 0
+
+    def across_x(c):
+        fwd, back = pltpu.roll(c, 127, 2), pltpu.roll(c, 1, 2)
+        fwd = jnp.where(at_end, jnp.concatenate([fwd[1:], fwd[:1]], axis=0), fwd)
+        back = jnp.where(at_start, jnp.concatenate([back[3:], back[:3]], axis=0), back)
+        return fwd - back
+
+    def get(f, l, r):
+        return big[f, l, :, r : r + 16, :]
+
+    def vertical(f, l, r):
+        up = get(f, jnp.minimum(l + 1, NL - 1), r) * jnp.where(l < NL - 1, 1.0, 0.0)
+        down = get(f, jnp.maximum(l - 1, 0), r) * jnp.where(l > 0, 1.0, 0.0)
+        return up - down
+
+    def winds(rows):
+        def body(l, _):
+            for r in rows:
+                ok = mask[:, r : r + 16, :]
+                big[U, l, :, r : r + 16, :] = (get(U, l, r) - 0.25 * across_x(get(PR, l, r))) * ok
+                along = get(PR, l, r + 1) - get(PR, l, r - 1)
+                big[V, l, :, r : r + 16, :] = (get(V, l, r) - 0.25 * along) * ok
+                big[W, l, :, r : r + 16, :] = get(W, l, r) - 0.25 * vertical(PR, l, r) + 0.5 * get(TH, l, r)
+            return 0
+
+        lax.fori_loop(0, NL, body, 0)
+
+    def pressure(rows, last=False):
+        def body(l, _):
+            for r in rows:
+                along = get(V, l, r + 1) - get(V, l, r - 1)
+                diverge = across_x(get(U, l, r)) + along + vertical(W, l, r)
+                new_p = get(PR, l, r) - 0.25 * get(SS, l, r) * diverge
+                new_t = get(TH, l, r) - 0.5 * get(W, l, r)
+                if last:
+                    done = (get(U, l, r), get(V, l, r), get(W, l, r), new_p, new_t)
+                    for f, cells in enumerate(done):
+                        for t in range(3):
+                            adv[f, l, r - TOP : r - TOP + 16, t * 128 : t * 128 + 128] = cells[t]
+                else:
+                    big[PR, l, :, r : r + 16, :] = new_p * mask[:, r : r + 16, :]
+                    big[TH, l, :, r : r + 16, :] = new_t
+            return 0
+
+        lax.fori_loop(0, NL, body, 0)
+
+    for d in far:
+        scatter(d).wait_recv()
+    total = half[pl.ds(pl.multiple_of(me * CHUNK, 8), CHUNK), :]
+    for d in range(1, 16):
+        total = total + xy_recv[d]
+    red[...] = total
+
+    def across(d):
+        return remote(red, z_recv.at[d], z_send.at[d], z_got.at[d], column_dev(d))
+
+    for d in deep:
+        across(d).start()
 
     for copy in x_copies:
         copy.wait()
@@ -284,18 +350,12 @@
     for copy in c_copies:
         copy.start()
 
-    for d in far:
-        scatter(d).wait_recv()
-    total = half[pl.ds(pl.multiple_of(me * CHUNK, 8), CHUNK), :]
-    for d in range(1, 16):
-        total = total + xy_recv[d]
-    red[...] = total
-
-    def across(d):
-        return remote(red, z_recv.at[d], z_send.at[d], z_got.at[d], column_dev(d))
-
-    for d in deep:
-        across(d).start()
+    def mask_p(l, _):
+        big[PR, l, 3, TOP:BOT, :] = big[PR, l, 3, TOP:BOT, :] * mask[3, TOP:BOT, :]
+        return 0
+
+    lax.fori_loop(0, NL, mask_p, 0)
+    winds((24, 40, 56))
     for d in deep:
         across(d).wait_recv()
     total = red[...]
@@ -357,69 +417,23 @@
 
     lax.fori_loop(0, 6, unpack_c, 0)
 
-    def mask_p(l, _):
-        big[PR, l, 3, 8:88, :] = big[PR, l, 3, 8:88, :] * mask[3, 8:88, :]
-        return 0
-
-    lax.fori_loop(0, NL, mask_p, 0)
-
-    lane4 = lanes((4, 16, 128))
-    at_end, at_start = lane4 == 127, lane4 == 0
-
-    def across_x(c):
-        fwd, back = pltpu.roll(c, 127, 2), pltpu.roll(c, 1, 2)
-        fwd = jnp.where(at_end, jnp.concatenate([fwd[1:], fwd[:1]], axis=0), fwd)
-        back = jnp.where(at_start, jnp.concatenate([back[3:], back[:3]], axis=0), back)
-        return fwd - back
-
-    def get(f, l, r):
-        return big[f, l, :, r : r + 16, :]
-
-    def vertical(f, l, r):
-        up = get(f, jnp.minimum(l + 1, NL - 1), r) * jnp.where(l < NL - 1, 1.0, 0.0)
-        down = get(f, jnp.maximum(l - 1, 0), r) * jnp.where(l > 0, 1.0, 0.0)
-        return up - down
-
-    def winds(l, _):
-        for r in range(8, 88, 16):
-            ok = mask[:, r : r + 16, :]
-            big[U, l, :, r : r + 16, :] = (get(U, l, r) - 0.25 * across_x(get(PR, l, r))) * ok
-            along = get(PR, l, r + 1) - get(PR, l, r - 1)
-            big[V, l, :, r : r + 16, :] = (get(V, l, r) - 0.25 * along) * ok
-            big[W, l, :, r : r + 16, :] = get(W, l, r) - 0.25 * vertical(PR, l, r) + 0.5 * get(TH, l, r)
-        return 0
-
-    def pressure(rows):
-        def body(l, _):
-            for r in rows:
-                along = get(V, l, r + 1) - get(V, l, r - 1)
-                diverge = across_x(get(U, l, r)) + along + vertical(W, l, r)
-                new_p = (get(PR, l, r) - 0.25 * get(SS, l, r) * diverge) * mask[:, r : r + 16, :]
-                big[PR, l, :, r : r + 16, :] = new_p
-                big[TH, l, :, r : r + 16, :] = get(TH, l, r) - 0.5 * get(W, l, r)
-            return 0
-
-        return body
-
-    def put_out(first, count, t, k):
-        return pltpu.make_async_copy(
-            big.at[pl.ds(first, count), :, t, pl.ds(TOP, ROWS), :],
-            adv.at[pl.ds(first, count), :, :, pl.ds(t * 128, 128)],
-            out_sem.at[k, t],
-        )
-
-    for step in range(SUBSTEPS):
-        last = step == SUBSTEPS - 1
-        lax.fori_loop(0, NL, winds, 0)
-        if last:
-            for t in range(3):
-                put_out(0, 3, t, 0).start()
-            for d in far:
-                gather(d).wait_recv()
-                forward(d).start()
-        lax.fori_loop(0, NL, pressure(range(TOP, BOT, 16) if last else range(8, 88, 16)), 0)
-    for t in range(3):
-        put_out(3, 2, t, 1).start()
+    def mask_c(l, _):
+        for r in (TOP - 8, BOT):
+            big[PR, l, 3, r : r + 8, :] = big[PR, l, 3, r : r + 8, :] * mask[3, r : r + 8, :]
+        return 0
+
+    lax.fori_loop(0, NL, mask_c, 0)
+
+    every = range(8, 88, 16)
+    winds((8, 72))
+    pressure(every)
+    winds(every)
+    pressure(every)
+    winds(every)
+    for d in far:
+        gather(d).wait_recv()
+        forward(d).start()
+    pressure(range(TOP, BOT, 16), last=True)
 
     for d in range(16):
         forward(d).wait()
@@ -428,14 +442,11 @@
         gather(d).wait_send()
     for d in deep:
         across(d).wait_send()
-    for t in range(3):
-        put_out(0, 3, t, 0).wait()
-        put_out(3, 2, t, 1).wait()
 
 
 def sum_modes(state, driving, sound, tab_x, tab_y):
     vmem = pl.BlockSpec(memory_space=pltpu.VMEM)
-    hbm = pl.BlockSpec(memory_space=pl.ANY)
+    hbm = pl.BlockSpec(memory_space=pltpu.HBM)
     dma = pltpu.SemaphoreType.DMA
     return pl.pallas_call(
         mode_kernel,
@@ -446,7 +457,7 @@
             jax.ShapeDtypeStruct((64, 256), BF16),
         ),
         in_specs=[hbm] * 5,
-        out_specs=(vmem, hbm, vmem, vmem),
+        out_specs=(vmem, vmem, vmem, vmem),
         scratch_shapes=[
             pltpu.VMEM((6, NL, 4, 96, 128), F32),
             pltpu.VMEM((NF, NL, ROWS, COLS), F32),
@@ -470,13 +481,13 @@
             dma((NF, 3)), dma((NF,)), dma((3,)), dma((2,)), dma((2,)),
             dma((16,)), dma((16,)), dma((8,)), dma((8,)),
             dma((16,)), dma((16,)), dma((16,)), dma((16,)),
-            dma((2,)), dma((2,)), dma((2,)), dma((2,)), dma((2,)), dma((2,)), dma((2, 3)),
+            dma((2,)), dma((2,)), dma((2,)), dma((2,)), dma((2,)), dma((2,)),
         ],
         compiler_params=pltpu.CompilerParams(
-            collective_id=0, has_side_effects=True, vmem_limit_bytes=48 * 1024 * 1024
+            collective_id=0, has_side_effects=True, vmem_limit_bytes=40 * 1024 * 1024
         ),
         name="sum_modes",
-    )(state, driving, sound, tab_x, tab_y)
+    )(*(pltpu.with_memory_space_constraint(a, pltpu.HBM) for a in (state, driving, sound, tab_x, tab_y)))
 
 
 def back_kernel(rate, modes, xt3, yt3, adv, out):

time: 53.5 us -> 48.3 us (0.903)
  local copies, waits for them, and re-layouts: 5.6 us -> 0.01 us
  Pallas kernels: 47.6 us -> 48.3 us
    unnamed x10 -> x2, local copies, waits for them, and re-layouts: 5.6 us -> 0.01 us
    pallas_call x1, Pallas kernels: 42.7 us -> 43.3 us  [sum_modes(): pl.pallas_call(mode_kernel, out_shape=(jax.ShapeDtypeStruct((2 * HALF, 12...]
where the time goes in v2:
time: 48.3 us
  Pallas kernels  48.3 us (100%)
    pallas_call x1, Pallas kernels, sum_modes(): pl.pallas_call(mode_kernel, out_shape=(jax.ShapeDtypeStruct((2 * HALF, 12...  43.3 us
    pallas_call x1, Pallas kernels, nudge(): pl.pallas_call(back_kernel, grid=(NF,), out_shape=jax.ShapeDtypeStruct((N...  4.97 us

profile of v2, /device:TPU:1, one launch (start us, length us, event | category | flops | bytes accessed | tf_op | source)
XLA Modules:
  0.0 48.3 jit_solution(17622585337711744170)
XLA Ops:
  0.0 0.0 copy-start
  0.0 43.3 %sum_modes.1 = (f32[1280,128]{1,0:T(8,128)S(1)}, f32[5,8,64,384]{3,2,1,0:T(8,128)S(1)}, bf16[384,384]{1,0:T(8,128)(2,1)S(1)}, bf16[64,256]{1,0:T(8,128)(2,1)S(1)}) custom-call(f32[5,8,64,384]{3,2,1,0:T(8,128)} %state.1, f32[5,8,64,384]{3,2,1,0:T(8,128)} %driving.1, f32[8,64,384]{2,1,0:T(8,128)} %sound.1, f32[8,64,384]{2,1,0:T(8,128)} %constant.4.clone.tab_x, ...), custom_call_target="tpu_custom_call" | custom-call | tf_op jit(solution)/shard_map/sum_modes/pallas_call | solution.py:451
  43.3 0.0 copy-done
  43.3 5.0 %nudge.1 = f32[5,8,64,384]{3,2,1,0:T(8,128)} custom-call(f32[5,8]{1,0:T(8,128)S(1)} %copy-done, f32[20,64,128]{2,1,0:T(8,128)S(1)} %bitcast.1, bf16[384,384]{1,0:T(8,128)(2,1)S(1)} %get-tuple-element.10.xt3, bf16[64,256]{1,0:T(8,128)(2,1)S(1)} %get-tuple-element.11.yt3, f32[5,8,64,384]{3,2,1,0:T(8,128)S(1)} %get-tuple-element.12.adv), custom_call_target="tpu_custom_call" | custom-call | tf_op jit(solution)/shard_map/nudge/pallas_call | solution.py:511
Async XLA Ops:
  0.0 43.3 %copy-start = (f32[5,8]{1,0:T(8,128)S(1)}, f32[5,8]{1,0:T(8,128)}, u32[]{:S(2)}) copy-start(f32[5,8]{1,0:T(8,128)} %rate.1) | copy-start | bytes 484

commit v3 on v2

--- a/solution.py
+++ b/solution.py
@@ -16,6 +16,7 @@
 MESH = pl.DeviceIdType.MESH
 TOP, BOT = 16, 80
 HALF, CHUNK = 640, 40
+UNROLL = 2
 U, V, W, PR, TH, SS = range(6)
 
 
@@ -216,6 +217,25 @@
         return 0
 
     lax.fori_loop(0, 6, pack_x, 0)
+    low_rows = lax.broadcasted_iota(jnp.int32, (3, 8, 128), 1) < 4
+
+    def pack_y(l, _):
+        for s, r in ((0, TOP), (1, BOT - 8)):
+            def strip(f):
+                return big[f, l, 0:3, r : r + 8, :]
+
+            def joined(a, b):
+                if s == 0:
+                    return jnp.where(low_rows, strip(a), pltpu.roll(strip(b), 4, 1))
+                return jnp.where(low_rows, pltpu.roll(strip(a), 4, 1), strip(b))
+
+            ys[s, l, 0] = strip(PR)
+            ys[s, l, 1] = strip(V)
+            ys[s, l, 2] = joined(U, W)
+            ys[s, l, 3] = joined(TH, SS)
+        return 0
+
+    lax.fori_loop(0, NL, pack_y, 0)
     give.wait()
     half[...] = local[pl.ds(pl.multiple_of(core * HALF, 8), HALF), :] + core_recv[...]
 
@@ -229,31 +249,12 @@
     for d in far:
         scatter(d).start()
 
+    y_copies = [remote(ys.at[s], yr.at[s], yh_send.at[s], yh_got.at[s], rows_to[s]) for s in range(2)]
+    for copy in y_copies:
+        copy.start()
+
     x_copies = [remote(xs.at[s], xr.at[s], xh_send.at[s], xh_got.at[s], sides[s]) for s in range(2)]
     for copy in x_copies:
-        copy.start()
-
-    low_rows = lax.broadcasted_iota(jnp.int32, (3, 8, 128), 1) < 4
-
-    def pack_y(l, _):
-        for s, r in ((0, TOP), (1, BOT - 8)):
-            def strip(f):
-                return big[f, l, 0:3, r : r + 8, :]
-
-            def joined(a, b):
-                if s == 0:
-                    return jnp.where(low_rows, strip(a), pltpu.roll(strip(b), 4, 1))
-                return jnp.where(low_rows, pltpu.roll(strip(a), 4, 1), strip(b))
-
-            ys[s, l, 0] = strip(PR)
-            ys[s, l, 1] = strip(V)
-            ys[s, l, 2] = joined(U, W)
-            ys[s, l, 3] = joined(TH, SS)
-        return 0
-
-    lax.fori_loop(0, NL, pack_y, 0)
-    y_copies = [remote(ys.at[s], yr.at[s], yh_send.at[s], yh_got.at[s], rows_to[s]) for s in range(2)]
-    for copy in y_copies:
         copy.start()
 
     lane4 = lanes((4, 16, 128))
@@ -283,7 +284,7 @@
                 big[W, l, :, r : r + 16, :] = get(W, l, r) - 0.25 * vertical(PR, l, r) + 0.5 * get(TH, l, r)
             return 0
 
-        lax.fori_loop(0, NL, body, 0)
+        lax.fori_loop(0, NL, body, 0, unroll=UNROLL)
 
     def pressure(rows, last=False):
         def body(l, _):
@@ -302,7 +303,7 @@
                     big[TH, l, :, r : r + 16, :] = new_t
             return 0
 
-        lax.fori_loop(0, NL, body, 0)
+        lax.fori_loop(0, NL, body, 0, unroll=UNROLL)
 
     for d in far:
         scatter(d).wait_recv()
@@ -490,39 +491,44 @@
     )(*(pltpu.with_memory_space_constraint(a, pltpu.HBM) for a in (state, driving, sound, tab_x, tab_y)))
 
 
-def back_kernel(rate, modes, xt3, yt3, adv, out):
-    f = pl.program_id(0)
+def back_kernel(rate, modes, xt3, yt3, adv, out, held, done, sem):
     side = lanes((64, 128)) < 64
-    scaled = [modes[q] * jnp.where(side, rate[f, 2 * q], rate[f, 2 * q + 1]) for q in range(4)]
-    high, low = split(jnp.concatenate(scaled, axis=1))
-    back = dot(yt3[...], jnp.concatenate([high, high, low, low], axis=0))
-    rows = []
-    for q in range(4):
-        both = back[:, 128 * q : 128 * q + 128]
-        rows += [jnp.where(side, both, 0.0), jnp.where(side, 0.0, both)]
-    high, low = split(jnp.concatenate(rows, axis=0))
-    tendency = dot(jnp.concatenate([high, low, high], axis=1), xt3[...])
-    out[0] = adv[0] - tendency.reshape(NL, ROWS, COLS)
+    for f in range(NF):
+        scaled = [
+            modes[4 * f + q] * jnp.where(side, rate[f, 2 * q], rate[f, 2 * q + 1]) for q in range(4)
+        ]
+        high, low = split(jnp.concatenate(scaled, axis=1))
+        held[f] = dot(yt3[...], jnp.concatenate([high, high, low, low], axis=0))
+
+    def write(f):
+        return pltpu.make_async_copy(done.at[f], out.at[f], sem.at[f])
+
+    for f in range(NF):
+        rows = []
+        for q in range(4):
+            both = held[f, :, 128 * q : 128 * q + 128]
+            rows += [jnp.where(side, both, 0.0), jnp.where(side, 0.0, both)]
+        high, low = split(jnp.concatenate(rows, axis=0))
+        tendency = dot(jnp.concatenate([high, low, high], axis=1), xt3[...])
+        done[f] = adv[f] - tendency.reshape(NL, ROWS, COLS)
+        write(f).start()
+    for f in range(NF):
+        write(f).wait()
 
 
 def nudge(rate, modes, xt3, yt3, adv):
-    block = pl.BlockSpec((1, NL, ROWS, COLS), lambda f: (f, 0, 0, 0))
     vmem = pl.BlockSpec(memory_space=pltpu.VMEM)
     return pl.pallas_call(
         back_kernel,
-        grid=(NF,),
         out_shape=jax.ShapeDtypeStruct((NF, NL, ROWS, COLS), F32),
-        in_specs=[
-            pl.BlockSpec(memory_space=pltpu.SMEM),
-            pl.BlockSpec((4, 64, 128), lambda f: (f, 0, 0)),
-            vmem,
-            vmem,
-            block,
+        in_specs=[pl.BlockSpec(memory_space=pltpu.SMEM)] + [vmem] * 4,
+        out_specs=pl.BlockSpec(memory_space=pltpu.HBM),
+        scratch_shapes=[
+            pltpu.VMEM((NF, 64, 512), F32),
+            pltpu.VMEM((NF, NL, ROWS, COLS), F32),
+            pltpu.SemaphoreType.DMA((NF,)),
         ],
-        out_specs=block,
-        compiler_params=pltpu.CompilerParams(
-            dimension_semantics=("arbitrary",), vmem_limit_bytes=24 * 1024 * 1024
-        ),
+        compiler_params=pltpu.CompilerParams(vmem_limit_bytes=32 * 1024 * 1024),
         name="nudge",
     )(rate, modes, xt3, yt3, adv)
 

time: 48.3 us -> 46 us (0.952)
  Pallas kernels: 48.3 us -> 46 us
    pallas_call x1, Pallas kernels: 4.97 us -> 3.19 us  [nudge(): pl.pallas_call(back_kernel, out_shape=jax.ShapeDtypeStruct((NF, NL, ROWS,...]
    pallas_call x1, Pallas kernels: 43.3 us -> 42.8 us  [sum_modes(): pl.pallas_call(mode_kernel, out_shape=(jax.ShapeDtypeStruct((2 * HALF, 12...]
where the time goes in v3:
time: 46 us
  Pallas kernels  46 us (100%)
    pallas_call x1, Pallas kernels, sum_modes(): pl.pallas_call(mode_kernel, out_shape=(jax.ShapeDtypeStruct((2 * HALF, 12...  42.8 us
    pallas_call x1, Pallas kernels, nudge(): pl.pallas_call(back_kernel, out_shape=jax.ShapeDtypeStruct((NF, NL, ROWS,...  3.19 us

profile of v3, /device:TPU:1, one launch (start us, length us, event | category | flops | bytes accessed | tf_op | source)
XLA Modules:
  0.0 46.0 jit_solution(996078919475884749)
XLA Ops:
  0.0 0.0 copy-start
  0.0 42.8 %sum_modes.1 = (f32[1280,128]{1,0:T(8,128)S(1)}, f32[5,8,64,384]{3,2,1,0:T(8,128)S(1)}, bf16[384,384]{1,0:T(8,128)(2,1)S(1)}, bf16[64,256]{1,0:T(8,128)(2,1)S(1)}) custom-call(f32[5,8,64,384]{3,2,1,0:T(8,128)} %state.1, f32[5,8,64,384]{3,2,1,0:T(8,128)} %driving.1, f32[8,64,384]{2,1,0:T(8,128)} %sound.1, f32[8,64,384]{2,1,0:T(8,128)} %constant.4.clone.tab_x, ...), custom_call_target="tpu_custom_call" | custom-call | tf_op jit(solution)/shard_map/sum_modes/pallas_call | solution.py:452
  42.8 0.0 copy-done
  42.8 3.2 %nudge.1 = f32[5,8,64,384]{3,2,1,0:T(8,128)} custom-call(f32[5,8]{1,0:T(8,128)S(1)} %copy-done, f32[20,64,128]{2,1,0:T(8,128)S(1)} %bitcast.1, bf16[384,384]{1,0:T(8,128)(2,1)S(1)} %get-tuple-element.10.xt3, bf16[64,256]{1,0:T(8,128)(2,1)S(1)} %get-tuple-element.11.yt3, f32[5,8,64,384]{3,2,1,0:T(8,128)S(1)} %get-tuple-element.12.adv), custom_call_target="tpu_custom_call" | custom-call | tf_op jit(solution)/shard_map/nudge/pallas_call | solution.py:521
Async XLA Ops:
  0.0 42.8 %copy-start = (f32[5,8]{1,0:T(8,128)S(1)}, f32[5,8]{1,0:T(8,128)}, u32[]{:S(2)}) copy-start(f32[5,8]{1,0:T(8,128)} %rate.1) | copy-start | bytes 484

commit v4 on v3

--- a/solution.py
+++ b/solution.py
@@ -217,22 +217,36 @@
         return 0
 
     lax.fori_loop(0, 6, pack_x, 0)
-    low_rows = lax.broadcasted_iota(jnp.int32, (3, 8, 128), 1) < 4
+    sub = lax.broadcasted_iota(jnp.int32, (3, 8, 128), 1)
+    low_rows = sub < 4
+
+    def edge(f, l, r):
+        return big[f, l, 0:3, r : r + 8, :]
+
+    def edge_z(l, r):
+        up = edge(PR, jnp.minimum(l + 1, NL - 1), r) * jnp.where(l < NL - 1, 1.0, 0.0)
+        down = edge(PR, jnp.maximum(l - 1, 0), r) * jnp.where(l > 0, 1.0, 0.0)
+        return up - down
 
     def pack_y(l, _):
         for s, r in ((0, TOP), (1, BOT - 8)):
-            def strip(f):
-                return big[f, l, 0:3, r : r + 8, :]
-
             def joined(a, b):
                 if s == 0:
-                    return jnp.where(low_rows, strip(a), pltpu.roll(strip(b), 4, 1))
-                return jnp.where(low_rows, pltpu.roll(strip(a), 4, 1), strip(b))
-
-            ys[s, l, 0] = strip(PR)
-            ys[s, l, 1] = strip(V)
-            ys[s, l, 2] = joined(U, W)
-            ys[s, l, 3] = joined(TH, SS)
+                    return jnp.where(low_rows, a, pltpu.roll(b, 4, 1))
+                return jnp.where(low_rows, pltpu.roll(a, 4, 1), b)
+
+            w_1 = edge(W, l, r) - 0.25 * edge_z(l, r) + 0.5 * edge(TH, l, r)
+            t_1 = edge(TH, l, r) - 0.5 * w_1
+            v_0 = edge(V, l, r)
+            v_1 = v_0 - 0.25 * (edge(PR, l, r + 1) - edge(PR, l, r - 1))
+            first = sub == (0 if s == 0 else 7)
+            v = jnp.where(first, v_0, v_1)
+            ys[s, l, 0] = joined(edge(U, l, r), w_1)
+            ys[s, l, 1] = joined(edge(PR, l, r), edge(SS, l, r))
+            if s == 0:
+                ys[s, l, 2] = jnp.where(sub < 5, v, pltpu.roll(t_1, 5, 1))
+            else:
+                ys[s, l, 2] = jnp.where(sub >= 3, v, pltpu.roll(t_1, 2, 1))
         return 0
 
     lax.fori_loop(0, NL, pack_y, 0)
@@ -385,30 +399,36 @@
     for copy in c_copies:
         copy.wait()
 
+    def put(f, l, r, cells):
+        big[f, l, 0:3, r : r + 8, :] = cells
+
+    def other(cells):
+        return pltpu.roll(cells, 4, 1)
+
     def unpack_y(l, _):
         for s, r in ((0, BOT), (1, TOP - 8)):
-            def put(f, cells):
-                big[f, l, 0:3, r : r + 8, :] = cells
-
-            def other(cells):
-                return pltpu.roll(cells, 4, 1)
-
-            put(PR, yr[s, l, 0] * mask[0:3, r : r + 8, :])
-            put(V, yr[s, l, 1])
-            one, two = yr[s, l, 2], yr[s, l, 3]
-            if s == 0:
-                put(U, one)
-                put(W, other(one))
-                put(TH, two)
-                put(SS, other(two))
-            else:
-                put(U, other(one))
-                put(W, one)
-                put(TH, other(two))
-                put(SS, two)
+            near_four = low_rows if s == 0 else sub >= 4
+            one, two = yr[s, l, 0], yr[s, l, 1]
+            put(U, l, r, one if s == 0 else other(one))
+            p = two if s == 0 else other(two)
+            put(PR, l, r, jnp.where(near_four, p, 0.0) * mask[0:3, r : r + 8, :])
+            put(SS, l, r, other(two) if s == 0 else two)
+        return 0
+
+    def unpack_first(l, _):
+        for s, r in ((0, BOT), (1, TOP - 8)):
+            one, three = yr[s, l, 0], yr[s, l, 2]
+            w_1 = other(one) if s == 0 else one
+            t_1 = pltpu.roll(three, 3 if s == 0 else 6, 1)
+            theta = jnp.where((sub < 2) if s == 0 else (sub >= 6), t_1 + 0.5 * w_1, 0.0)
+            put(TH, l, r, theta)
+            put(W, l, r, w_1 + 0.25 * edge_z(l, r) - 0.5 * theta)
+            along = edge(PR, l, r + 1) - edge(PR, l, r - 1)
+            put(V, l, r, jnp.where(sub == (0 if s == 0 else 7), three, three + 0.25 * along))
         return 0
 
     lax.fori_loop(0, NL, unpack_y, 0)
+    lax.fori_loop(0, NL, unpack_first, 0)
 
     def unpack_c(f, _):
         for s, r in ((0, BOT), (1, TOP - 8)):
@@ -475,8 +495,8 @@
             pltpu.VMEM((8, CHUNK, 128), F32),
             pltpu.VMEM((2, 6, 32, 128), F32),
             pltpu.VMEM((2, 6, 32, 128), F32),
-            pltpu.VMEM((2, NL, 4, 3, 8, 128), F32),
-            pltpu.VMEM((2, NL, 4, 3, 8, 128), F32),
+            pltpu.VMEM((2, NL, 3, 3, 8, 128), F32),
+            pltpu.VMEM((2, NL, 3, 3, 8, 128), F32),
             pltpu.VMEM((2, 6, 8, 128), F32),
             pltpu.VMEM((2, 6, 8, 128), F32),
             dma((NF, 3)), dma((NF,)), dma((3,)), dma((2,)), dma((2,)),

time: 46 us -> 44.3 us (0.963)
  Pallas kernels: 46 us -> 44.2 us
    pallas_call x1, Pallas kernels: 42.8 us -> 41 us  [sum_modes(): pl.pallas_call(mode_kernel, out_shape=(jax.ShapeDtypeStruct((2 * HALF, 12...]
where the time goes in v4:
time: 44.3 us; the launch traced here: 44.2 us
  Pallas kernels  44.2 us (100%)
    pallas_call x1, Pallas kernels, sum_modes(): pl.pallas_call(mode_kernel, out_shape=(jax.ShapeDtypeStruct((2 * HALF, 12...  41 us
    pallas_call x1, Pallas kernels, nudge(): pl.pallas_call(back_kernel, out_shape=jax.ShapeDtypeStruct((NF, NL, ROWS,...  3.19 us

profile of v4, /device:TPU:1, one launch (start us, length us, event | category | flops | bytes accessed | tf_op | source)
XLA Modules:
  0.0 44.2 jit_solution(1332798878056587433)
XLA Ops:
  0.0 0.0 copy-start
  0.0 41.0 %sum_modes.1 = (f32[1280,128]{1,0:T(8,128)S(1)}, f32[5,8,64,384]{3,2,1,0:T(8,128)S(1)}, bf16[384,384]{1,0:T(8,128)(2,1)S(1)}, bf16[64,256]{1,0:T(8,128)(2,1)S(1)}) custom-call(f32[5,8,64,384]{3,2,1,0:T(8,128)} %state.1, f32[5,8,64,384]{3,2,1,0:T(8,128)} %driving.1, f32[8,64,384]{2,1,0:T(8,128)} %sound.1, f32[8,64,384]{2,1,0:T(8,128)} %constant.4.clone.tab_x, ...), custom_call_target="tpu_custom_call" | custom-call | tf_op jit(solution)/shard_map/sum_modes/pallas_call | solution.py:472
  41.0 0.0 copy-done
  41.0 3.2 %nudge.1 = f32[5,8,64,384]{3,2,1,0:T(8,128)} custom-call(f32[5,8]{1,0:T(8,128)S(1)} %copy-done, f32[20,64,128]{2,1,0:T(8,128)S(1)} %bitcast.1, bf16[384,384]{1,0:T(8,128)(2,1)S(1)} %get-tuple-element.10.xt3, bf16[64,256]{1,0:T(8,128)(2,1)S(1)} %get-tuple-element.11.yt3, f32[5,8,64,384]{3,2,1,0:T(8,128)S(1)} %get-tuple-element.12.adv), custom_call_target="tpu_custom_call" | custom-call | tf_op jit(solution)/shard_map/nudge/pallas_call | solution.py:541
Async XLA Ops:
  0.0 41.0 %copy-start = (f32[5,8]{1,0:T(8,128)S(1)}, f32[5,8]{1,0:T(8,128)}, u32[]{:S(2)}) copy-start(f32[5,8]{1,0:T(8,128)} %rate.1) | copy-start | bytes 484

commit v5 on v4

--- a/solution.py
+++ b/solution.py
@@ -99,6 +99,35 @@
 
     far = sorted(range(1, 16), key=lambda d: -(min(d % 4, 4 - d % 4) + min(d // 4, 4 - d // 4)))
     deep = sorted(range(1, 8), key=lambda d: -min(d, 8 - d))
+
+    inner = {"x": (gx > 0, gx < GX - 1), "y": (gy > 0, gy < GY - 1), "c": (gy > 0, gy < GY - 1)}
+
+    @pl.when(gx == GX - 1)
+    def _():
+        xr[0] = jnp.zeros_like(xr[0])
+
+    @pl.when(gx == 0)
+    def _():
+        xr[1] = jnp.zeros_like(xr[1])
+
+    @pl.when(gy == GY - 1)
+    def _():
+        yr[0] = jnp.zeros_like(yr[0])
+        cr[0] = jnp.zeros_like(cr[0])
+
+    @pl.when(gy == 0)
+    def _():
+        yr[1] = jnp.zeros_like(yr[1])
+        cr[1] = jnp.zeros_like(cr[1])
+
+    def start_bands(name, copies):
+        for s in range(2):
+            pl.when(inner[name][s])(copies[s].start)
+
+    def wait_bands(name, copies):
+        for s in range(2):
+            pl.when(inner[name][s])(copies[s].wait_send)
+            pl.when(inner[name][1 - s])(copies[s].wait_recv)
 
     barrier = pltpu.get_barrier_semaphore()
     peers = [partner] + [plane_dev(d) for d in far] + [column_dev(d) for d in deep]
@@ -253,6 +282,9 @@
     give.wait()
     half[...] = local[pl.ds(pl.multiple_of(core * HALF, 8), HALF), :] + core_recv[...]
 
+    y_copies = [remote(ys.at[s], yr.at[s], yh_send.at[s], yh_got.at[s], rows_to[s]) for s in range(2)]
+    start_bands("y", y_copies)
+
     def scatter(d):
         x, y = plane(d)
         return remote(
@@ -263,13 +295,8 @@
     for d in far:
         scatter(d).start()
 
-    y_copies = [remote(ys.at[s], yr.at[s], yh_send.at[s], yh_got.at[s], rows_to[s]) for s in range(2)]
-    for copy in y_copies:
-        copy.start()
-
     x_copies = [remote(xs.at[s], xr.at[s], xh_send.at[s], xh_got.at[s], sides[s]) for s in range(2)]
-    for copy in x_copies:
-        copy.start()
+    start_bands("x", x_copies)
 
     lane4 = lanes((4, 16, 128))
     at_end, at_start = lane4 == 127, lane4 == 0
@@ -332,8 +359,7 @@
     for d in deep:
         across(d).start()
 
-    for copy in x_copies:
-        copy.wait()
+    wait_bands("x", x_copies)
     near = lanes((32, 128)) < 64
 
     def unpack_x(f, _):
@@ -362,8 +388,7 @@
 
     lax.fori_loop(0, 6, pack_c, 0)
     c_copies = [remote(cs.at[s], cr.at[s], ch_send.at[s], ch_got.at[s], rows_to[s]) for s in range(2)]
-    for copy in c_copies:
-        copy.start()
+    start_bands("c", c_copies)
 
     def mask_p(l, _):
         big[PR, l, 3, TOP:BOT, :] = big[PR, l, 3, TOP:BOT, :] * mask[3, TOP:BOT, :]
@@ -394,10 +419,8 @@
         gather(d).start()
     forward(0).start()
 
-    for copy in y_copies:
-        copy.wait()
-    for copy in c_copies:
-        copy.wait()
+    wait_bands("y", y_copies)
+    wait_bands("c", c_copies)
 
     def put(f, l, r, cells):
         big[f, l, 0:3, r : r + 8, :] = cells

time: 44.3 us -> 41.8 us (0.944)
  Pallas kernels: 44.2 us -> 41.7 us
    pallas_call x1, Pallas kernels: 41 us -> 38.5 us  [sum_modes(): pl.pallas_call(mode_kernel, out_shape=(jax.ShapeDtypeStruct((2 * HALF, 12...]
where the time goes in v5:
time: 41.8 us; the launch traced here: 41.7 us
  Pallas kernels  41.7 us (100%)
    pallas_call x1, Pallas kernels, sum_modes(): pl.pallas_call(mode_kernel, out_shape=(jax.ShapeDtypeStruct((2 * HALF, 12...  38.5 us
    pallas_call x1, Pallas kernels, nudge(): pl.pallas_call(back_kernel, out_shape=jax.ShapeDtypeStruct((NF, NL, ROWS,...  3.19 us

profile of v5, /device:TPU:1, one launch (start us, length us, event | category | flops | bytes accessed | tf_op | source)
XLA Modules:
  0.0 41.7 jit_solution(16090161978782788255)
XLA Ops:
  0.0 0.0 copy-start
  0.0 38.5 %sum_modes.1 = (f32[1280,128]{1,0:T(8,128)S(1)}, f32[5,8,64,384]{3,2,1,0:T(8,128)S(1)}, bf16[384,384]{1,0:T(8,128)(2,1)S(1)}, bf16[64,256]{1,0:T(8,128)(2,1)S(1)}) custom-call(f32[5,8,64,384]{3,2,1,0:T(8,128)} %state.1, f32[5,8,64,384]{3,2,1,0:T(8,128)} %driving.1, f32[8,64,384]{2,1,0:T(8,128)} %sound.1, f32[8,64,384]{2,1,0:T(8,128)} %constant.4.clone.tab_x, ...), custom_call_target="tpu_custom_call" | custom-call | tf_op jit(solution)/shard_map/sum_modes/pallas_call | solution.py:495
  38.5 0.0 copy-done
  38.5 3.2 %nudge.1 = f32[5,8,64,384]{3,2,1,0:T(8,128)} custom-call(f32[5,8]{1,0:T(8,128)S(1)} %copy-done, f32[20,64,128]{2,1,0:T(8,128)S(1)} %bitcast.1, bf16[384,384]{1,0:T(8,128)(2,1)S(1)} %get-tuple-element.10.xt3, bf16[64,256]{1,0:T(8,128)(2,1)S(1)} %get-tuple-element.11.yt3, f32[5,8,64,384]{3,2,1,0:T(8,128)S(1)} %get-tuple-element.12.adv), custom_call_target="tpu_custom_call" | custom-call | tf_op jit(solution)/shard_map/nudge/pallas_call | solution.py:564
Async XLA Ops:
  0.0 38.5 %copy-start = (f32[5,8]{1,0:T(8,128)S(1)}, f32[5,8]{1,0:T(8,128)}, u32[]{:S(2)}) copy-start(f32[5,8]{1,0:T(8,128)} %rate.1) | copy-start | bytes 484

commit v6 on v5

--- a/solution.py
+++ b/solution.py
@@ -232,20 +232,6 @@
 
     for t in range(3):
         load_sound(t).wait()
-    slot = lanes((32, 128)) // 8
-
-    def pack_x(f, _):
-        for side, tile in ((0, 0), (1, 2)):
-            acc = None
-            for i in range(16):
-                cells = big[f, i // 2, tile, TOP + 32 * (i % 2) : TOP + 32 * (i % 2) + 32, :]
-                shift = (8 * (i + side)) % 128
-                cells = pltpu.roll(cells, shift, 1) if shift else cells
-                acc = cells if acc is None else jnp.where(slot == i, cells, acc)
-            xs[side, f] = acc
-        return 0
-
-    lax.fori_loop(0, 6, pack_x, 0)
     sub = lax.broadcasted_iota(jnp.int32, (3, 8, 128), 1)
     low_rows = sub < 4
 
@@ -279,11 +265,25 @@
         return 0
 
     lax.fori_loop(0, NL, pack_y, 0)
+    y_copies = [remote(ys.at[s], yr.at[s], yh_send.at[s], yh_got.at[s], rows_to[s]) for s in range(2)]
+    start_bands("y", y_copies)
+
+    slot = lanes((32, 128)) // 8
+
+    def pack_x(f, _):
+        for side, tile in ((0, 0), (1, 2)):
+            acc = None
+            for i in range(16):
+                cells = big[f, i // 2, tile, TOP + 32 * (i % 2) : TOP + 32 * (i % 2) + 32, :]
+                shift = (8 * (i + side)) % 128
+                cells = pltpu.roll(cells, shift, 1) if shift else cells
+                acc = cells if acc is None else jnp.where(slot == i, cells, acc)
+            xs[side, f] = acc
+        return 0
+
+    lax.fori_loop(0, 6, pack_x, 0)
     give.wait()
     half[...] = local[pl.ds(pl.multiple_of(core * HALF, 8), HALF), :] + core_recv[...]
-
-    y_copies = [remote(ys.at[s], yr.at[s], yh_send.at[s], yh_got.at[s], rows_to[s]) for s in range(2)]
-    start_bands("y", y_copies)
 
     def scatter(d):
         x, y = plane(d)

time: 41.8 us -> 43.3 us (1.036)
  the two profiles are of different devices: /device:TPU:1 before, /device:TPU:79 now
where the time goes in v6:
time: 43.3 us; the launch traced here: 43.2 us
  Pallas kernels  43.2 us (100%)
    pallas_call x1, Pallas kernels, sum_modes(): pl.pallas_call(mode_kernel, out_shape=(jax.ShapeDtypeStruct((2 * HALF, 12...  40 us
    pallas_call x1, Pallas kernels, nudge(): pl.pallas_call(back_kernel, out_shape=jax.ShapeDtypeStruct((NF, NL, ROWS,...  3.19 us

profile of v6, /device:TPU:79, one launch (start us, length us, event | category | flops | bytes accessed | tf_op | source)
XLA Modules:
  0.0 43.2 jit_solution(279919087651023182)
XLA Ops:
  0.0 0.0 copy-start
  0.0 40.0 %sum_modes.1 = (f32[1280,128]{1,0:T(8,128)S(1)}, f32[5,8,64,384]{3,2,1,0:T(8,128)S(1)}, bf16[384,384]{1,0:T(8,128)(2,1)S(1)}, bf16[64,256]{1,0:T(8,128)(2,1)S(1)}) custom-call(f32[5,8,64,384]{3,2,1,0:T(8,128)} %state.1, f32[5,8,64,384]{3,2,1,0:T(8,128)} %driving.1, f32[8,64,384]{2,1,0:T(8,128)} %sound.1, f32[8,64,384]{2,1,0:T(8,128)} %constant.4.clone.tab_x, ...), custom_call_target="tpu_custom_call" | custom-call | tf_op jit(solution)/shard_map/sum_modes/pallas_call | solution.py:495
  40.0 0.0 copy-done
  40.1 3.2 %nudge.1 = f32[5,8,64,384]{3,2,1,0:T(8,128)} custom-call(f32[5,8]{1,0:T(8,128)S(1)} %copy-done, f32[20,64,128]{2,1,0:T(8,128)S(1)} %bitcast.1, bf16[384,384]{1,0:T(8,128)(2,1)S(1)} %get-tuple-element.10.xt3, bf16[64,256]{1,0:T(8,128)(2,1)S(1)} %get-tuple-element.11.yt3, f32[5,8,64,384]{3,2,1,0:T(8,128)S(1)} %get-tuple-element.12.adv), custom_call_target="tpu_custom_call" | custom-call | tf_op jit(solution)/shard_map/nudge/pallas_call | solution.py:564
Async XLA Ops:
  0.0 40.0 %copy-start = (f32[5,8]{1,0:T(8,128)S(1)}, f32[5,8]{1,0:T(8,128)}, u32[]{:S(2)}) copy-start(f32[5,8]{1,0:T(8,128)} %rate.1) | copy-start | bytes 484
